TPU v7x, 512 devices: a 4x2x32 block of a 4x8x32 slice. The times are simulated.
512 devices in a mesh: groups: 2 (over y), rows: 32 (over z), keys: 4 (over x), heads: 2 (over core).
Axes of the slice: x: 4, y: 2, z: 32, core: 2. Of those that a mesh axis runs over, the one named last changes fastest.
The devices are a block of a 4x8x32 slice.
Arguments:
- pair: bfloat16 [2048, 1024, 128], P(('groups', 'rows'), 'keys'), parts along dimension 0, may hold values from -6 to 6
- seq_length: int32 [2], P('groups'), parts along dimension 0, may hold values from 513 to 1024
- tile_counts: int32 [2048, 8], P(('groups', 'rows')), parts along dimension 0, may hold values from 0 to 128, as said below
- ln_gain: float32 [128], replicated, may hold values from 0.5 to 1.5
- w_query: bfloat16 [128, 128], P(None, 'heads'), may hold values from -8 to 8
- w_key: bfloat16 [128, 128], P(None, 'heads'), may hold values from -0.5 to 0.5
- w_value: bfloat16 [128, 128], P(None, 'heads'), may hold values from -0.5 to 0.5
- w_gate: bfloat16 [128, 128], P(None, 'heads'), may hold values from -0.5 to 0.5
- w_bias: bfloat16 [128, 4], P(None, 'heads'), may hold values from -1.5 to 1.5
- w_out: bfloat16 [128, 128], replicated, may hold values from -2 to 2
Outputs:
- update: bfloat16 [2048, 1024, 128], P(('groups', 'rows'), ('keys', 'heads')), parts along dimension 0
There are 2 independent parts, one for each index of `groups`. A program takes and returns all parts, laid end to end along the dimension named above; an argument that names none is the same for every part. Nothing has to cross between parts.
Inputs may be any that keep to these rules, and one draw needn't show every extreme that they name: `tile_counts`: for each row and each tile of 128 keys, how many of the tile's leading keys are valid; some rows have no valid key at all.
All inputs are finite; a program needn't handle non-finite values.
Results may differ from a plain program's by a relative error of at most 0.03.
The roundings to bfloat16 on the way count: a program that leaves them out, or rounds other values in their place, can miss the bound.
Values may be sent and summed in bfloat16 or wider, within the bound.
A program may use at most 128 MiB of HBM per device.

v0:
```python
import jax
import jax.numpy as jnp
from jax import lax
from jax.sharding import PartitionSpec as P

HEAD_DIM = 32
TILE = 128


norm_epsilon = 1e-05
masked_score = -1e30


def from_everyone(value, axis):
    peers = lax.axis_size(axis)
    return lax.all_to_all(
        jnp.broadcast_to(value[None], (peers, *value.shape)), axis, 0, 0, tiled=True
    )


def laid_out(tiles, dim):
    tiles = jnp.moveaxis(tiles, 0, dim)
    dims = tiles.shape
    return tiles.reshape(*dims[:dim], dims[dim] * dims[dim + 1], *dims[dim + 2 :])


def gathered_copies(value, axis, dim):
    tiles = from_everyone(value, axis)
    return laid_out(tiles, dim)


def sent_together(arrays, axis, dim, along):
    ends, at = ([], 0)
    for a in arrays[:-1]:
        at += a.shape[along]
        ends.append(at)
    both = jnp.concatenate(arrays, axis=along)
    return tuple(jnp.split(lax.all_gather(both, axis, axis=dim, tiled=True), ends, axis=along))


def exchange_in_groups(value, axis, split_dim, concat_dim, work, item_dim, out_dim):
    items = jax.tree.leaves(value)[0].shape[item_dim]
    count = 2 if items % 2 == 0 else 1
    done = []
    for k in range(count):
        group = jax.tree.map(
            lambda a: lax.slice_in_dim(
                a, k * (items // count), (k + 1) * (items // count), axis=item_dim
            ),
            value,
        )
        done.append(
            work(
                lax.all_to_all(
                    group, axis, split_axis=split_dim, concat_axis=concat_dim, tiled=True
                )
            )
        )
    return jax.tree.map(lambda *parts: jnp.concatenate(parts, axis=out_dim), *done)


def layer_norm(values, gain):
    center = values - jnp.mean(values, axis=-1, keepdims=True)
    spread = jnp.mean(center * center, axis=-1, keepdims=True)
    return center * lax.rsqrt(spread + norm_epsilon) * gain


def finish(row_sum, weighted):
    denom = jnp.maximum(row_sum, 1.0)
    result = weighted / denom[..., None]
    rows_dev, heads_dev, cols_dev, depth = result.shape
    result = jnp.transpose(result, (0, 2, 1, 3)).reshape(rows_dev, cols_dev, heads_dev * depth)
    return result.astype(jnp.bfloat16)


def per_device(
    pair, seq_length, tile_counts, ln_gain, w_query, w_key, w_value, w_gate, w_bias, w_out
):
    rows_dev, cols_dev, channels = pair.shape
    key_groups = lax.axis_size("keys")
    length_all = cols_dev * key_groups
    heads_dev = w_bias.shape[1]
    width_dev = heads_dev * HEAD_DIM
    normed = layer_norm(pair.astype(jnp.float32), ln_gain).astype(jnp.bfloat16)
    flat = normed.reshape(rows_dev * cols_dev, channels)
    queries = (
        (jnp.dot(flat, w_query, preferred_element_type=jnp.float32) * HEAD_DIM ** (-0.5))
        .astype(jnp.bfloat16)
        .reshape(rows_dev, cols_dev, heads_dev, HEAD_DIM)
    )
    keys_local = (
        jnp.dot(flat, w_key, preferred_element_type=jnp.float32)
        .astype(jnp.bfloat16)
        .reshape(rows_dev, cols_dev, heads_dev, HEAD_DIM)
    )
    values_local = (
        jnp.dot(flat, w_value, preferred_element_type=jnp.float32)
        .astype(jnp.bfloat16)
        .reshape(rows_dev, cols_dev, heads_dev, HEAD_DIM)
    )
    gate_act = jax.nn.sigmoid(jnp.dot(flat, w_gate, preferred_element_type=jnp.float32)).reshape(
        rows_dev, cols_dev, width_dev
    )
    bias_local = jnp.einsum("rkc,ch->hrk", normed, w_bias, preferred_element_type=jnp.float32)
    bias_rows = gathered_copies(bias_local.astype(jnp.bfloat16), "rows", 1).astype(bias_local.dtype)
    positions = jnp.arange(length_all, dtype=jnp.int32)
    allowed = (positions[None, :] < seq_length[0]) & (
        (positions % TILE)[None, :] < jnp.repeat(tile_counts, TILE, axis=1)
    )
    bias_turn = lax.all_to_all(
        bias_rows.astype(jnp.bfloat16), "keys", split_axis=1, concat_axis=2, tiled=True
    ).astype(bias_rows.dtype)
    initial = (
        jnp.full((rows_dev, heads_dev, cols_dev), masked_score, jnp.float32),
        jnp.zeros((rows_dev, heads_dev, cols_dev), jnp.float32),
        jnp.zeros((rows_dev, heads_dev, cols_dev, HEAD_DIM), jnp.float32),
    )
    piece_keys, piece_values = sent_together((keys_local, values_local), "keys", 1, 0)

    def one_tile(tile_index, state):
        row_max, row_sum, weighted = state
        offset = tile_index * TILE
        key_tile = lax.dynamic_slice_in_dim(piece_keys, offset, TILE, 1)
        value_tile = lax.dynamic_slice_in_dim(piece_values, offset, TILE, 1)
        tile_bias = lax.dynamic_slice_in_dim(bias_turn, offset, TILE, 2)
        shown = lax.dynamic_slice_in_dim(allowed, offset, TILE, 1)[:, None, None, :]
        scores = (
            jnp.einsum("rjhd,rkhd->rhjk", queries, key_tile, preferred_element_type=jnp.float32)
            + tile_bias[None]
        )
        scores = jnp.where(shown, scores, masked_score)
        new_max = jnp.maximum(row_max, jnp.max(scores, axis=-1))
        weights = jnp.where(shown, jnp.exp(scores - new_max[..., None]), 0.0)
        rescale = jnp.exp(row_max - new_max)
        row_sum = row_sum * rescale + jnp.sum(weights, axis=-1)
        weighted = weighted * rescale[..., None] + jnp.einsum(
            "rhjk,rkhd->rhjd",
            weights.astype(jnp.bfloat16),
            value_tile,
            preferred_element_type=jnp.float32,
        )
        return (new_max, row_sum, weighted)

    row_max, row_sum, weighted = lax.fori_loop(0, piece_keys.shape[1] // TILE, one_tile, initial)
    attended = finish(row_sum, weighted)
    attended = lax.optimization_barrier(attended).astype(jnp.float32)
    gated = (gate_act * attended).astype(jnp.bfloat16)

    def project(mixed):
        return jnp.einsum("rkc,cd->rkd", mixed, w_out, preferred_element_type=jnp.float32).astype(
            jnp.bfloat16
        )

    return exchange_in_groups(gated, "heads", 1, 2, project, 0, 0)


def solution(mesh):
    in_specs = (
        P(("groups", "rows"), "keys", None),
        P("groups"),
        P(("groups", "rows"), None),
        P(),
        P(None, "heads"),
        P(None, "heads"),
        P(None, "heads"),
        P(None, "heads"),
        P(None, "heads"),
        P(),
    )
    out_specs = P(("groups", "rows"), ("keys", "heads"), None)
    return jax.shard_map(
        per_device, mesh=mesh, in_specs=in_specs, out_specs=out_specs, check_vma=False
    )
```

profile of v0, /device:TPU:33, one launch (start us, length us, event | category | flops | bytes accessed | tf_op | source)
XLA Modules:
  0.0 321.6 jit_solution(10131734697609890808)
XLA Ops:
  6.6 2.4 convert_reduce_fusion
  9.0 2.4 fusion.25
  11.4 2.5 fusion.27
  17.3 1.5 pad_maximum_fusion
  20.2 1.1 broadcast_in_dim.74
  21.3 46.3 %all-to-all-start = ((bf16[32,2,32,256]{3,2,1,0:T(8,128)(2,1)}), bf16[32,2,32,256]{3,2,1,0:T(8,128)(2,1)}, u32[]{:S(2)}, u32[]{:S(2)}) async-start(bf16[32,2,32,256]{3,2,1,0:T(8,128)(2,1)} %broadcast_in_dim.74), calls=%async_computation | async-start | bytes 2097152 | tf_op jit(solution)/shard_map/all_to_all | solution.py:16
  69.1 103.0 %all-to-all-done = bf16[32,2,32,256]{3,2,1,0:T(8,128)(2,1)} async-done(((bf16[32,2,32,256]{3,2,1,0:T(8,128)(2,1)}), bf16[32,2,32,256]{3,2,1,0:T(8,128)(2,1)}, u32[]{:S(2)}, u32[]{:S(2)}) %all-to-all-start) | async-done | bytes 1048608 | tf_op jit(solution)/shard_map/all_to_all | solution.py:16
  172.1 1.3 copy.64
  173.4 2.0 copy.65
  175.5 4.5 %all-to-all-start.1 = ((bf16[2,1024,256]{2,0,1:T(2,128)(2,1)}), bf16[2,1024,256]{2,0,1:T(2,128)(2,1)}, u32[]{:S(2)}, u32[]{:S(2)}) async-start(bf16[2,1024,256]{2,0,1:T(2,128)(2,1)} %copy.65), calls=%async_computation.1 | async-start | bytes 2097152 | tf_op jit(solution)/shard_map/all_to_all | solution.py:110
  181.1 2.2 fusion.21
  183.4 10.9 %all-to-all-done.1 = bf16[2,1024,256]{2,0,1:T(2,128)(2,1)} async-done(((bf16[2,1024,256]{2,0,1:T(2,128)(2,1)}), bf16[2,1024,256]{2,0,1:T(2,128)(2,1)}, u32[]{:S(2)}, u32[]{:S(2)}) %all-to-all-start.1) | async-done | bytes 1048608 | tf_op jit(solution)/shard_map/all_to_all | solution.py:110
  194.2 1.4 copy.66
  195.8 1.8 copy.67
  197.7 6.4 %fusion.37 = (bf16[32,1024,2,32]{1,3,2,0:T(8,128)(2,1)}, bf16[32,1024,2,32]{1,3,2,0:T(8,128)(2,1)}) fusion(bf16[64,1024,2,32]{1,3,2,0:T(8,128)(2,1)} %all-gather.2.cloned.1.call-done), kind=kLoop, calls=%fused_computation.63 | loop fusion | bytes 16777216 | tf_op jit(solution)/shard_map/split | solution.py:38
  204.0 90.0 %while.18 = (s32[]{:T(128)}, f32[32,2,256]{2,1,0:T(2,128)S(1)}, f32[32,2,256]{2,1,0:T(2,128)S(1)}, f32[32,2,256,32]{2,3,1,0:T(8,128)S(1)}, pred[32,1024]{1,0:T(8...) while((s32[]{:T(128)}, f32[32,2,256]{2,1,0:T(2,128)S(1)}, ...), condition=%wide.region_5.6_spmd.clone, body=%wide.region_2.5_spmd.clone.sunk | while | flops 297353216 | bytes 33837260 | solution.py:144
  204.1 1.0 constant_dynamic-slice_fusion.4
  205.0 3.4 %fusion.62 = (f32[32,2,256]{2,1,0:T(2,128)S(1)}, f32[32,2,128,256]{3,2,1,0:T(8,128)S(1)}) fusion(f32[2,256,128]{1,2,0:T(8,128)S(1)} %constant_dynamic-slice_fusion.4, pred[32,128]{1,0:T(8,128)(4,1)S(1)} %constant_dynamic-slice_fusion.5, bf16[32,256,2,32]{1,3,2,0:T(8,128)(2,1)S(1)} %get-tuple-element.358, ...), kind=kOutput, calls=%fused_computation.3.clone.1 | convolution fusion | flops 140492800 | bytes 10293252 | tf_op jit(solution)/shard_map/while/body/eval_jaxpr/rjhd,rkhd->rhjk/dot_general | solution.py:128
  208.5 3.0 fusion.64
  211.6 3.6 %fusion.66 = f32[32,2,256,32]{2,3,1,0:T(8,128)S(1)} fusion(f32[32,2,256,32]{2,3,1,0:T(8,128)S(1)} %get-tuple-element.342, f32[32,2,128,256]{3,2,1,0:T(8,128)S(1)} %get-tuple-element.323, f32[32,2,256]{2,1,0:T(2,128)S(1)} %fusion.63, f32[2,256,128]{1,2,0:T(8,128)S(1)} %constant_dynamic-slice_fusion.4, ...), kind=kOutput, calls=%fused_computation.9.clone.1 | convolution fusion | flops 146276352 | bytes 13504517 | tf_op jit(solution)/shard_map/while/body/eval_jaxpr/rhjk,rkhd->rhjd/dot_general | solution.py:136
  216.3 3.4 %fusion.62 = (f32[32,2,256]{2,1,0:T(2,128)S(1)}, f32[32,2,128,256]{3,2,1,0:T(8,128)S(1)}) fusion(f32[2,256,128]{1,2,0:T(8,128)S(1)} %constant_dynamic-slice_fusion.4, pred[32,128]{1,0:T(8,128)(4,1)S(1)} %constant_dynamic-slice_fusion.5, bf16[32,256,2,32]{1,3,2,0:T(8,128)(2,1)S(1)} %get-tuple-element.358, ...), kind=kOutput, calls=%fused_computation.3.clone.1 | convolution fusion | flops 140492800 | bytes 10293252 | tf_op jit(solution)/shard_map/while/body/eval_jaxpr/rjhd,rkhd->rhjk/dot_general | solution.py:128
  219.7 3.0 fusion.64
  222.9 3.6 %fusion.66 = f32[32,2,256,32]{2,3,1,0:T(8,128)S(1)} fusion(f32[32,2,256,32]{2,3,1,0:T(8,128)S(1)} %get-tuple-element.342, f32[32,2,128,256]{3,2,1,0:T(8,128)S(1)} %get-tuple-element.323, f32[32,2,256]{2,1,0:T(2,128)S(1)} %fusion.63, f32[2,256,128]{1,2,0:T(8,128)S(1)} %constant_dynamic-slice_fusion.4, ...), kind=kOutput, calls=%fused_computation.9.clone.1 | convolution fusion | flops 146276352 | bytes 13504517 | tf_op jit(solution)/shard_map/while/body/eval_jaxpr/rhjk,rkhd->rhjd/dot_general | solution.py:136
  226.6 1.0 constant_dynamic-slice_fusion.4
  227.5 3.4 %fusion.62 = (f32[32,2,256]{2,1,0:T(2,128)S(1)}, f32[32,2,128,256]{3,2,1,0:T(8,128)S(1)}) fusion(f32[2,256,128]{1,2,0:T(8,128)S(1)} %constant_dynamic-slice_fusion.4, pred[32,128]{1,0:T(8,128)(4,1)S(1)} %constant_dynamic-slice_fusion.5, bf16[32,256,2,32]{1,3,2,0:T(8,128)(2,1)S(1)} %get-tuple-element.358, ...), kind=kOutput, calls=%fused_computation.3.clone.1 | convolution fusion | flops 140492800 | bytes 10293252 | tf_op jit(solution)/shard_map/while/body/eval_jaxpr/rjhd,rkhd->rhjk/dot_general | solution.py:128
  231.0 3.0 fusion.64
  234.1 3.6 %fusion.66 = f32[32,2,256,32]{2,3,1,0:T(8,128)S(1)} fusion(f32[32,2,256,32]{2,3,1,0:T(8,128)S(1)} %get-tuple-element.342, f32[32,2,128,256]{3,2,1,0:T(8,128)S(1)} %get-tuple-element.323, f32[32,2,256]{2,1,0:T(2,128)S(1)} %fusion.63, f32[2,256,128]{1,2,0:T(8,128)S(1)} %constant_dynamic-slice_fusion.4, ...), kind=kOutput, calls=%fused_computation.9.clone.1 | convolution fusion | flops 146276352 | bytes 13504517 | tf_op jit(solution)/shard_map/while/body/eval_jaxpr/rhjk,rkhd->rhjd/dot_general | solution.py:136
  237.8 1.0 constant_dynamic-slice_fusion.4
  238.8 3.4 %fusion.62 = (f32[32,2,256]{2,1,0:T(2,128)S(1)}, f32[32,2,128,256]{3,2,1,0:T(8,128)S(1)}) fusion(f32[2,256,128]{1,2,0:T(8,128)S(1)} %constant_dynamic-slice_fusion.4, pred[32,128]{1,0:T(8,128)(4,1)S(1)} %constant_dynamic-slice_fusion.5, bf16[32,256,2,32]{1,3,2,0:T(8,128)(2,1)S(1)} %get-tuple-element.358, ...), kind=kOutput, calls=%fused_computation.3.clone.1 | convolution fusion | flops 140492800 | bytes 10293252 | tf_op jit(solution)/shard_map/while/body/eval_jaxpr/rjhd,rkhd->rhjk/dot_general | solution.py:128
  242.2 3.0 fusion.64
  245.4 3.6 %fusion.66 = f32[32,2,256,32]{2,3,1,0:T(8,128)S(1)} fusion(f32[32,2,256,32]{2,3,1,0:T(8,128)S(1)} %get-tuple-element.342, f32[32,2,128,256]{3,2,1,0:T(8,128)S(1)} %get-tuple-element.323, f32[32,2,256]{2,1,0:T(2,128)S(1)} %fusion.63, f32[2,256,128]{1,2,0:T(8,128)S(1)} %constant_dynamic-slice_fusion.4, ...), kind=kOutput, calls=%fused_computation.9.clone.1 | convolution fusion | flops 146276352 | bytes 13504517 | tf_op jit(solution)/shard_map/while/body/eval_jaxpr/rhjk,rkhd->rhjd/dot_general | solution.py:136
  250.0 3.4 %fusion.62 = (f32[32,2,256]{2,1,0:T(2,128)S(1)}, f32[32,2,128,256]{3,2,1,0:T(8,128)S(1)}) fusion(f32[2,256,128]{1,2,0:T(8,128)S(1)} %constant_dynamic-slice_fusion.4, pred[32,128]{1,0:T(8,128)(4,1)S(1)} %constant_dynamic-slice_fusion.5, bf16[32,256,2,32]{1,3,2,0:T(8,128)(2,1)S(1)} %get-tuple-element.358, ...), kind=kOutput, calls=%fused_computation.3.clone.1 | convolution fusion | flops 140492800 | bytes 10293252 | tf_op jit(solution)/shard_map/while/body/eval_jaxpr/rjhd,rkhd->rhjk/dot_general | solution.py:128
  253.5 3.0 fusion.64
  256.6 3.6 %fusion.66 = f32[32,2,256,32]{2,3,1,0:T(8,128)S(1)} fusion(f32[32,2,256,32]{2,3,1,0:T(8,128)S(1)} %get-tuple-element.342, f32[32,2,128,256]{3,2,1,0:T(8,128)S(1)} %get-tuple-element.323, f32[32,2,256]{2,1,0:T(2,128)S(1)} %fusion.63, f32[2,256,128]{1,2,0:T(8,128)S(1)} %constant_dynamic-slice_fusion.4, ...), kind=kOutput, calls=%fused_computation.9.clone.1 | convolution fusion | flops 146276352 | bytes 13504517 | tf_op jit(solution)/shard_map/while/body/eval_jaxpr/rhjk,rkhd->rhjd/dot_general | solution.py:136
  260.3 1.0 constant_dynamic-slice_fusion.4
  261.3 3.4 %fusion.62 = (f32[32,2,256]{2,1,0:T(2,128)S(1)}, f32[32,2,128,256]{3,2,1,0:T(8,128)S(1)}) fusion(f32[2,256,128]{1,2,0:T(8,128)S(1)} %constant_dynamic-slice_fusion.4, pred[32,128]{1,0:T(8,128)(4,1)S(1)} %constant_dynamic-slice_fusion.5, bf16[32,256,2,32]{1,3,2,0:T(8,128)(2,1)S(1)} %get-tuple-element.358, ...), kind=kOutput, calls=%fused_computation.3.clone.1 | convolution fusion | flops 140492800 | bytes 10293252 | tf_op jit(solution)/shard_map/while/body/eval_jaxpr/rjhd,rkhd->rhjk/dot_general | solution.py:128
  264.7 3.0 fusion.64
  267.9 3.6 %fusion.66 = f32[32,2,256,32]{2,3,1,0:T(8,128)S(1)} fusion(f32[32,2,256,32]{2,3,1,0:T(8,128)S(1)} %get-tuple-element.342, f32[32,2,128,256]{3,2,1,0:T(8,128)S(1)} %get-tuple-element.323, f32[32,2,256]{2,1,0:T(2,128)S(1)} %fusion.63, f32[2,256,128]{1,2,0:T(8,128)S(1)} %constant_dynamic-slice_fusion.4, ...), kind=kOutput, calls=%fused_computation.9.clone.1 | convolution fusion | flops 146276352 | bytes 13504517 | tf_op jit(solution)/shard_map/while/body/eval_jaxpr/rhjk,rkhd->rhjd/dot_general | solution.py:136
  272.5 3.4 %fusion.62 = (f32[32,2,256]{2,1,0:T(2,128)S(1)}, f32[32,2,128,256]{3,2,1,0:T(8,128)S(1)}) fusion(f32[2,256,128]{1,2,0:T(8,128)S(1)} %constant_dynamic-slice_fusion.4, pred[32,128]{1,0:T(8,128)(4,1)S(1)} %constant_dynamic-slice_fusion.5, bf16[32,256,2,32]{1,3,2,0:T(8,128)(2,1)S(1)} %get-tuple-element.358, ...), kind=kOutput, calls=%fused_computation.3.clone.1 | convolution fusion | flops 140492800 | bytes 10293252 | tf_op jit(solution)/shard_map/while/body/eval_jaxpr/rjhd,rkhd->rhjk/dot_general | solution.py:128
  276.0 3.0 fusion.64
  279.1 3.6 %fusion.66 = f32[32,2,256,32]{2,3,1,0:T(8,128)S(1)} fusion(f32[32,2,256,32]{2,3,1,0:T(8,128)S(1)} %get-tuple-element.342, f32[32,2,128,256]{3,2,1,0:T(8,128)S(1)} %get-tuple-element.323, f32[32,2,256]{2,1,0:T(2,128)S(1)} %fusion.63, f32[2,256,128]{1,2,0:T(8,128)S(1)} %constant_dynamic-slice_fusion.4, ...), kind=kOutput, calls=%fused_computation.9.clone.1 | convolution fusion | flops 146276352 | bytes 13504517 | tf_op jit(solution)/shard_map/while/body/eval_jaxpr/rhjk,rkhd->rhjd/dot_general | solution.py:136
  283.8 3.4 %fusion.62 = (f32[32,2,256]{2,1,0:T(2,128)S(1)}, f32[32,2,128,256]{3,2,1,0:T(8,128)S(1)}) fusion(f32[2,256,128]{1,2,0:T(8,128)S(1)} %constant_dynamic-slice_fusion.4, pred[32,128]{1,0:T(8,128)(4,1)S(1)} %constant_dynamic-slice_fusion.5, bf16[32,256,2,32]{1,3,2,0:T(8,128)(2,1)S(1)} %get-tuple-element.358, ...), kind=kOutput, calls=%fused_computation.3.clone.1 | convolution fusion | flops 140492800 | bytes 10293252 | tf_op jit(solution)/shard_map/while/body/eval_jaxpr/rjhd,rkhd->rhjk/dot_general | solution.py:128
  287.2 3.0 fusion.64
  290.4 3.6 %fusion.66 = f32[32,2,256,32]{2,3,1,0:T(8,128)S(1)} fusion(f32[32,2,256,32]{2,3,1,0:T(8,128)S(1)} %get-tuple-element.342, f32[32,2,128,256]{3,2,1,0:T(8,128)S(1)} %get-tuple-element.323, f32[32,2,256]{2,1,0:T(2,128)S(1)} %fusion.63, f32[2,256,128]{1,2,0:T(8,128)S(1)} %constant_dynamic-slice_fusion.4, ...), kind=kOutput, calls=%fused_computation.9.clone.1 | convolution fusion | flops 146276352 | bytes 13504517 | tf_op jit(solution)/shard_map/while/body/eval_jaxpr/rhjk,rkhd->rhjd/dot_general | solution.py:136
  294.4 1.2 copy-done.3
  297.9 5.7 %all_to_all.50 = bf16[2,2,65536]{2,1,0:T(2,128)(2,1)S(1)} all-to-all(bf16[2,2,65536]{2,1,0:T(2,128)(2,1)S(1)} %reshape.73), channel_id=1, replica_groups=mesh['groups'=2,'rows'=32,'keys'=4,'heads'=2] {'heads'}, dimensions={0} | all-to-all | bytes 1048576 | tf_op jit(solution)/shard_map/all_to_all | solution.py:54
  307.1 4.2 %all_to_all.51 = bf16[2,2,65536]{2,1,0:T(2,128)(2,1)S(1)} all-to-all(bf16[2,2,65536]{2,1,0:T(2,128)(2,1)S(1)} %reshape.71), channel_id=1, replica_groups=mesh['groups'=2,'rows'=32,'keys'=4,'heads'=2] {'heads'}, dimensions={0} | all-to-all | bytes 1048576 | tf_op jit(solution)/shard_map/all_to_all | solution.py:54
  313.6 1.1 pad_maximum_fusion.1
  (100 shorter events, 20.8 us)
Async XLA Ops:
  6.5 306.4 %copy-start = (bf16[128,128]{1,0:T(8,128)(2,1)S(1)}, bf16[128,128]{1,0:T(8,128)(2,1)}, u32[]{:S(2)}) copy-start(bf16[128,128]{1,0:T(8,128)(2,1)} %param.21) | copy-start | bytes 98308
  6.6 2.4 copy-start.1
  6.6 4.8 %copy-start.9 = (f32[128]{0:T(128)S(1)}, f32[128]{0:T(128)}, u32[]{:S(2)}) copy-start(f32[128]{0:T(128)} %param.15) | copy-start | bytes 1540
  6.6 191.1 %all-gather.2.cloned.1.call-start = ((), (), s32[]{:S(2)}) async-start(), calls=%async_computation.4 | async-start | bytes 10485760 | tf_op jit(solution)/shard_map/all_gather | solution.py:38
  6.6 4.8 %copy-start.2 = (bf16[32,256,128]{2,1,0:T(8,128)(2,1)S(1)}, bf16[32,256,128]{2,1,0:T(8,128)(2,1)}, u32[]{:S(2)}) copy-start(bf16[32,256,128]{2,1,0:T(8,128)(2,1)} %param.12) | copy-start | bytes 6291460
  11.4 2.5 copy-start.5
  14.7 0.9 copy-start.6
  18.8 0.7 copy-start.10
  20.1 48.1 %copy-start.7 = (bf16[128,64]{0,1:T(8,128)(2,1)S(1)}, bf16[128,64]{0,1:T(8,128)(2,1)}, u32[]{:S(2)}) copy-start(bf16[128,64]{0,1:T(8,128)(2,1)} %param.16) | copy-start | bytes 49156
  21.3 150.9 %all-to-all-start = ((bf16[32,2,32,256]{3,2,1,0:T(8,128)(2,1)}), bf16[32,2,32,256]{3,2,1,0:T(8,128)(2,1)}, u32[]{:S(2)}, u32[]{:S(2)}) async-start(bf16[32,2,32,256]{3,2,1,0:T(8,128)(2,1)} %broadcast_in_dim.74), calls=%async_computation | async-start | bytes 2097152 | tf_op jit(solution)/shard_map/all_to_all | solution.py:16
  173.4 6.6 %copy-start.8 = (s32[32,8]{0,1:T(8,128)S(1)}, s32[32,8]{0,1:T(8,128)}, u32[]{:S(2)}) copy-start(s32[32,8]{0,1:T(8,128)} %param.14) | copy-start | bytes 3076
  175.5 18.8 %all-to-all-start.1 = ((bf16[2,1024,256]{2,0,1:T(2,128)(2,1)}), bf16[2,1024,256]{2,0,1:T(2,128)(2,1)}, u32[]{:S(2)}, u32[]{:S(2)}) async-start(bf16[2,1024,256]{2,0,1:T(2,128)(2,1)} %copy.65), calls=%async_computation.1 | async-start | bytes 2097152 | tf_op jit(solution)/shard_map/all_to_all | solution.py:110
  180.1 1.0 copy-start.11
  197.6 6.4 %copy-start.4 = (f32[32,2,256,32]{2,3,1,0:T(8,128)S(1)}, f32[32,2,256,32]{2,3,1,0:T(8,128)}, u32[]{:S(2)}) copy-start(f32[32,2,256,32]{2,3,1,0:T(8,128)} %custom-call.2) | copy-start | bytes 6291460
  294.0 1.6 copy-start.3
Sparse Core Ops, SparseCore 0:
  19.0 126.4 all-gather.1
where the time goes:
time: 323 us; the launch traced here: 322 us
  waiting for transfers between devices  114 us (35%)
  matrix products  62 us (19%)
  starting transfers between devices  50.8 us (16%)
  other arithmetic  36.3 us (11%)
  local copies, waits for them, and re-layouts  33.6 us (10%)
  between operations  14.5 us (4%)
  blocking collectives  9.84 us (3%)
    all_to_all x1, waiting for transfers between devices, from_everyone(): lax.all_to_all(jnp.broadcast_to(value[None], (peers, *value.shape)), axis...  103 us
    all_to_all x1, starting transfers between devices, from_everyone(): lax.all_to_all(jnp.broadcast_to(value[None], (peers, *value.shape)), axis...  46.3 us
    dot_general x8, matrix products, one_tile(): jnp.einsum('rhjk,rkhd->rhjd', weights.astype(jnp.bfloat16), value_tile, p...  28.9 us
    dot_general x8, matrix products, one_tile(): jnp.einsum('rjhd,rkhd->rhjk', queries, key_tile, preferred_element_type=j...  27 us
    reduce_sum x8, other arithmetic, one_tile(): row_sum = row_sum * rescale + jnp.sum(weights, axis=-1)  24 us
    all_to_all x1, waiting for transfers between devices, per_device(): lax.all_to_all(bias_rows.astype(jnp.bfloat16), 'keys', split_axis=1, conc...  10.9 us
    all_to_all x2, blocking collectives, exchange_in_groups(): lax.all_to_all(group, axis, split_axis=split_dim, concat_axis=concat_dim,...  9.84 us
    dynamic_slice x8, local copies, waits for them, and re-layouts, one_tile(): tile_bias = lax.dynamic_slice_in_dim(bias_turn, offset, TILE, 2)  7.84 us
  transfers between devices with their start and end apart: 3, of which 2 were waited for; matrix products, arithmetic and copies ran while one was open for 4% of the time, Pallas kernels for 0%

commit v1 on v0

v1 whole, which is shorter than its diff:
```python
import functools

import jax
import jax.numpy as jnp
from jax import lax
from jax.experimental import pallas as pl
from jax.experimental.pallas import tpu as pltpu
from jax.sharding import PartitionSpec as P

HEAD_DIM = 32
TILE = 128
norm_epsilon = 1e-05
masked_score = -1e30
CHUNKS = 8
MESH = pl.DeviceIdType.MESH
NT = (((1,), (1,)), ((), ()))
TN = (((0,), (0,)), ((), ()))


def nt(a, b):
    return lax.dot_general(a, b, NT, preferred_element_type=jnp.float32)


def exchange_kernel(
    pair_ref, gain_ref, wcat_ref, g_ref, bias_ref, wout_ref,
    xbuf, nbuf, wbuf, bpiece, bbuf,
    in_sem, w_send, w_recv, w_loc, b_send, b_recv, b_loc,
    z_recv, z_right, z_left,
    x_send, x_recv, y_send, y_recv, s_send, s_recv, g_loc, out_sem,
):
    x, c, r = lax.axis_index("keys"), lax.axis_index("heads"), lax.axis_index("rows")
    X, R = lax.axis_size("keys"), lax.axis_size("rows")
    rows, qdev, chan = nbuf.shape
    sources = bbuf.shape[0]
    pieces = 2 * X
    step = rows // CHUNKS
    half = step // 2
    mine = 2 * x + c
    xr, xl = lax.rem(x + 1, X), lax.rem(x + X - 1, X)
    zr, zl = lax.rem(r + 1, R), lax.rem(r + R - 1, R)
    sib = 1 - c

    load = pltpu.make_async_copy(pair_ref.at[:, pl.ds(pl.multiple_of(c * qdev, qdev), qdev), :], xbuf, in_sem)
    load.start()
    w_own = pltpu.make_async_copy(wcat_ref, wbuf.at[c], w_loc)
    w_own.start()

    barrier = pltpu.get_barrier_semaphore()
    for dx in range(X):
        for dc in range(2):
            if dx or dc:
                pl.semaphore_signal(
                    barrier, inc=1,
                    device_id={"keys": lax.rem(x + dx, X), "heads": lax.rem(c + dc, 2)},
                    device_id_type=MESH,
                )
    for z in (zr, zl):
        pl.semaphore_signal(barrier, inc=1, device_id={"rows": z}, device_id_type=MESH)
    pl.semaphore_wait(barrier, 2 * X - 1 + 2)

    def remote(src, dst, send, recv, where):
        return pltpu.make_async_remote_copy(
            src_ref=src, dst_ref=dst, send_sem=send, recv_sem=recv, device_id=where, device_id_type=MESH
        )

    w_copy = remote(wcat_ref, wbuf.at[c], w_send, w_recv, {"heads": sib})
    w_copy.start()
    load.wait()

    gain = gain_ref[...]

    def own_copies(m):
        at = pl.ds(m * step, step)
        src = nbuf.at[at]
        dst = g_ref.at[mine, at]
        return (
            remote(src, dst, x_send.at[0, m], x_recv.at[0, m], {"keys": xr}),
            remote(src, dst, x_send.at[1, m], x_recv.at[1, m], {"keys": xl}),
            remote(src, dst, x_send.at[2, m], x_recv.at[2, m], {"heads": sib}),
        )

    def send_own(m):
        for copy in own_copies(m):
            copy.start()
        pltpu.make_async_copy(nbuf.at[pl.ds(m * step, step)], g_ref.at[mine, pl.ds(m * step, step)], g_loc.at[m]).start()

    def norm_chunk(m, carry):
        at = pl.ds(m * step, step)
        v = xbuf[at].astype(jnp.float32)
        center = v - jnp.mean(v, axis=-1, keepdims=True)
        spread = jnp.mean(center * center, axis=-1, keepdims=True)
        nbuf[at] = (center * lax.rsqrt(spread + norm_epsilon) * gain[None]).astype(jnp.bfloat16)

        @pl.when(m > 0)
        def _():
            send_own(m - 1)

        return carry

    lax.fori_loop(0, CHUNKS, norm_chunk, 0)

    w_own.wait()
    w_copy.wait_recv()
    wb = jnp.concatenate([wbuf[0, 4], wbuf[1, 4]], axis=0).astype(jnp.float32)
    lane_row = lax.rem(lax.broadcasted_iota(jnp.int32, wb.shape, 0), rows)

    def bias_rows(n, acc):
        for k in range(4):
            j = n * 4 + k
            acc = acc + nt(nbuf[j], jnp.where(lane_row == j, wb, 0.0).astype(jnp.bfloat16))
        return acc

    acc = lax.fori_loop(0, rows // 4, bias_rows, jnp.zeros((qdev, 4 * rows), jnp.float32))
    bpiece[...] = acc.astype(jnp.bfloat16)
    send_own(CHUNKS - 1)

    block = (r * rows) // qdev
    a_me = lax.rem(r, sources)
    ox, oc = block // 2, lax.rem(block, 2)
    is_owner = block == mine

    def piece_at(a, p):
        return bbuf.at[a, pl.ds(p * qdev, qdev)]

    b_local = pltpu.make_async_copy(bpiece, piece_at(a_me, mine), b_loc)
    b_remote = remote(bpiece, piece_at(a_me, mine), b_send, b_recv.at[mine], {"keys": ox, "heads": oc})

    @pl.when(is_owner)
    def _():
        b_local.start()

    @pl.when(jnp.logical_not(is_owner))
    def _():
        b_remote.start()

    def to_right(a, p):
        return remote(piece_at(a, p), piece_at(a, p), z_right.at[a, p], z_recv.at[a, p], {"rows": zr})

    def to_left(a, p):
        return remote(piece_at(a, p), piece_at(a, p), z_left.at[a, p], z_recv.at[a, p], {"rows": zl})

    @pl.when(is_owner)
    def _():
        def own_piece(p, carry):
            @pl.when(p == mine)
            def _():
                b_local.wait()

            @pl.when(p != mine)
            def _():
                remote(bpiece, piece_at(a_me, p), b_send, b_recv.at[p], {"keys": ox, "heads": oc}).wait_recv()

            to_right(a_me, p).start()
            to_left(a_me, p).start()
            return carry

        lax.fori_loop(0, pieces, own_piece, 0)

    base = mine * sources
    middle = R // 2
    d0 = lax.rem(r - base + R, R)
    rightish = d0 <= middle + 1

    def place(n):
        t = n // pieces
        a = jnp.where(rightish, sources - 1 - t, t)
        return a, lax.rem(n, pieces), lax.rem(r - base - a + 2 * R, R)

    def z_time(n):
        _, _, d = place(n)
        hops = jnp.minimum(d, R - d)
        return 90 + 25 * hops + 7 * n

    def z_step(n):
        a, p, d = place(n)

        @pl.when(d != 0)
        def _():
            to_right(a, p).wait_recv()

            @pl.when(d < middle)
            def _():
                to_right(a, p).start()

            @pl.when(d > middle + 1)
            def _():
                to_left(a, p).start()

    left_piece, right_piece = 2 * xl + c, 2 * xr + c
    far_piece = 2 * lax.rem(x + 2, X) + c

    def forwards(m):
        lo, hi, at = pl.ds(m * step, half), pl.ds(m * step + half, half), pl.ds(m * step, step)
        return (
            remote(g_ref.at[left_piece, lo], g_ref.at[left_piece, lo], y_send.at[0, m], y_recv.at[0, m], {"keys": xr}),
            remote(g_ref.at[right_piece, hi], g_ref.at[right_piece, hi], y_send.at[1, m], y_recv.at[1, m], {"keys": xl}),
            remote(g_ref.at[left_piece, at], g_ref.at[left_piece, at], s_send.at[0, m], s_recv.at[0, m], {"heads": sib}),
            remote(g_ref.at[right_piece, at], g_ref.at[right_piece, at], s_send.at[1, m], s_recv.at[1, m], {"heads": sib}),
        )

    def far_copy(m):
        at = pl.ds(m * step, step)
        return remote(g_ref.at[far_piece, at], g_ref.at[far_piece, at], s_send.at[2, m], s_recv.at[2, m], {"heads": sib})

    def x_first(m):
        first, second, _ = own_copies(m)
        first.wait_recv()
        second.wait_recv()
        for copy in forwards(m):
            copy.start()

    def x_second(m):
        first, second, _, _ = forwards(m)
        first.wait_recv()
        second.wait_recv()
        far_copy(m).start()

    z_total = sources * pieces

    def x_time(n):
        return jnp.where(n < CHUNKS, 60 + 29 * (n + 1), 300 + 15 * (n - CHUNKS + 1))

    def merged(_, state):
        nz, nx = state
        use_x = jnp.logical_and(
            nx < 2 * CHUNKS, jnp.logical_or(nz >= z_total, x_time(nx) <= z_time(nz))
        )

        @pl.when(jnp.logical_and(use_x, nx < CHUNKS))
        def _():
            x_first(nx)

        @pl.when(jnp.logical_and(use_x, nx >= CHUNKS))
        def _():
            x_second(nx - CHUNKS)

        @pl.when(jnp.logical_not(use_x))
        def _():
            z_step(nz)

        took = use_x.astype(jnp.int32)
        return nz + 1 - took, nx + took

    lax.fori_loop(0, z_total + 2 * CHUNKS, merged, (0, 0))

    bias_out = pltpu.make_async_copy(bbuf, bias_ref, out_sem.at[0])
    w_out = pltpu.make_async_copy(wbuf, wout_ref, out_sem.at[1])
    bias_out.start()
    w_out.start()

    w_copy.wait_send()

    @pl.when(jnp.logical_not(is_owner))
    def _():
        b_remote.wait_send()

    def drain_z(n, carry):
        a, p, d = place(n)

        @pl.when(d < middle)
        def _():
            to_right(a, p).wait_send()

        @pl.when(jnp.logical_or(d == 0, d > middle + 1))
        def _():
            to_left(a, p).wait_send()

        return carry

    lax.fori_loop(0, z_total, drain_z, 0)

    def drain_x(m, carry):
        first, second, third = own_copies(m)
        for copy in (first, second, third):
            copy.wait_send()
        third.wait_recv()
        to_r, to_l, sib_l, sib_r = forwards(m)
        for copy in (to_r, to_l, sib_l, sib_r):
            copy.wait_send()
        sib_l.wait_recv()
        sib_r.wait_recv()
        far = far_copy(m)
        far.wait_send()
        far.wait_recv()
        pltpu.make_async_copy(nbuf.at[pl.ds(m * step, step)], g_ref.at[mine, pl.ds(m * step, step)], g_loc.at[m]).wait()
        return carry

    lax.fori_loop(0, CHUNKS, drain_x, 0)
    bias_out.wait()
    w_out.wait()


def exchange(pair, gain, wcat, key_groups, heads_axis):
    rows, cols, chan = pair.shape
    qdev = cols // heads_axis
    pieces = heads_axis * key_groups
    sources = qdev // rows
    length = qdev * pieces
    dma = pltpu.SemaphoreType.DMA
    any_spec = pl.BlockSpec(memory_space=pl.ANY)
    vmem = pl.BlockSpec(memory_space=pltpu.VMEM)
    bf16 = jnp.bfloat16
    return pl.pallas_call(
        exchange_kernel,
        name="exchange",
        out_shape=(
            jax.ShapeDtypeStruct((pieces, rows, qdev, chan), bf16),
            jax.ShapeDtypeStruct((sources, length, 4 * rows), bf16),
            jax.ShapeDtypeStruct((heads_axis, *wcat.shape), bf16),
        ),
        in_specs=[any_spec, vmem, vmem],
        out_specs=(any_spec, any_spec, any_spec),
        scratch_shapes=[
            pltpu.VMEM((rows, qdev, chan), bf16),
            pltpu.VMEM((rows, qdev, chan), bf16),
            pltpu.VMEM((heads_axis, *wcat.shape), bf16),
            pltpu.VMEM((qdev, 4 * rows), bf16),
            pltpu.VMEM((sources, length, 4 * rows), bf16),
            dma, dma, dma, dma, dma, dma((pieces,)), dma,
            dma((sources, pieces)), dma((sources, pieces)), dma((sources, pieces)),
            dma((3, CHUNKS)), dma((3, CHUNKS)), dma((2, CHUNKS)), dma((2, CHUNKS)),
            dma((3, CHUNKS)), dma((3, CHUNKS)), dma((CHUNKS,)), dma((2,)),
        ],
        compiler_params=pltpu.CompilerParams(collective_id=0, has_side_effects=True),
    )(pair, gain, wcat)


def attend_kernel(
    seq_ref, counts_ref, g_ref, bias_ref, w_ref, wout_ref, out_ref, bias32, keys_aug, q_bd
):
    i = pl.program_id(0)
    pieces, _, qdev, chan = g_ref.shape
    sources, length, lanes = bias_ref.shape
    rows = lanes // 4
    mine = 2 * lax.axis_index("keys") + lax.axis_index("heads")
    bf16, f32 = jnp.bfloat16, jnp.float32

    @pl.when(i == 0)
    def _():
        bias32[...] = bias_ref[...].astype(f32)
        q_bd[...] = jnp.zeros(q_bd.shape, bf16)
        first = lax.broadcasted_iota(jnp.int32, (16, sources * lanes), 0) == 0
        q_bd[chan:chan + 16, :] = jnp.where(first, 1.0, 0.0).astype(bf16)

    wq, wk, wv, wg = (jnp.concatenate([w_ref[0, k], w_ref[1, k]], axis=0) for k in range(4))
    rows_all = g_ref[...].reshape(length, chan)
    own = g_ref[mine, 0]

    keys_aug[:, :chan] = nt(rows_all, wk).astype(bf16)
    values_t = nt(wv, rows_all).astype(bf16)
    key_at = lax.broadcasted_iota(jnp.int32, (TILE, chan), 0)
    lane_at = lax.broadcasted_iota(jnp.int32, (TILE, chan), 1)
    for t in range(length // TILE):
        limit = jnp.minimum(counts_ref[i, t], seq_ref[0] - t * TILE)
        hit = jnp.logical_and(lane_at == 0, key_at >= limit)
        keys_aug[t * TILE:(t + 1) * TILE, chan:] = jnp.where(hit, masked_score, 0.0).astype(bf16)

    head_row = lax.broadcasted_iota(jnp.int32, (chan, lanes), 0) // HEAD_DIM
    head_lane = lax.broadcasted_iota(jnp.int32, (chan, lanes), 1) // rows
    diagonal = head_row == head_lane
    reps = [jnp.concatenate([own[a * rows:(a + 1) * rows]] * 4, axis=0) for a in range(sources)]
    for a in range(sources):
        qa = nt(wq, reps[a]) * HEAD_DIM ** (-0.5)
        q_bd[:chan, a * lanes:(a + 1) * lanes] = jnp.where(diagonal, qa, 0.0).astype(bf16)

    for b in range(sources // 2):
        cols = slice(2 * b * lanes, 2 * (b + 1) * lanes)
        scores = jnp.dot(keys_aug[...], q_bd[:, cols], preferred_element_type=f32)
        scores = scores + jnp.concatenate([bias32[2 * b], bias32[2 * b + 1]], axis=1)
        top = jnp.maximum(jnp.max(scores, axis=0, keepdims=True), masked_score * 0.1)
        weights = jnp.exp(scores - top)
        total = jnp.maximum(jnp.sum(weights, axis=0, keepdims=True), 1.0)
        mixed = jnp.dot(values_t, weights.astype(bf16), preferred_element_type=f32)
        attended = (mixed / total).astype(bf16).astype(f32)
        for k in range(2):
            a = 2 * b + k
            gate = jax.nn.sigmoid(nt(wg, reps[a]))
            gated = jnp.where(diagonal, gate * attended[:, k * lanes:(k + 1) * lanes], 0.0).astype(bf16)
            full = lax.dot_general(gated, wout_ref[...], TN, preferred_element_type=f32)
            summed = full[:rows] + full[rows:2 * rows] + full[2 * rows:3 * rows] + full[3 * rows:]
            out_ref[0, a * rows:(a + 1) * rows, :] = summed.astype(bf16)


def attend(seq_length, tile_counts, gathered, bias, weights, w_out):
    pieces, rows, qdev, chan = gathered.shape
    sources, length, lanes = bias.shape
    smem = pl.BlockSpec(memory_space=pltpu.SMEM)
    return pl.pallas_call(
        attend_kernel,
        name="attend",
        grid=(rows,),
        out_shape=jax.ShapeDtypeStruct((rows, qdev, chan), jnp.bfloat16),
        in_specs=[
            smem,
            smem,
            pl.BlockSpec((pieces, 1, qdev, chan), lambda i: (0, i, 0, 0)),
            pl.BlockSpec(bias.shape, lambda i: (0, 0, 0)),
            pl.BlockSpec(weights.shape, lambda i: (0, 0, 0, 0)),
            pl.BlockSpec(w_out.shape, lambda i: (0, 0)),
        ],
        out_specs=pl.BlockSpec((1, qdev, chan), lambda i: (i, 0, 0)),
        scratch_shapes=[
            pltpu.VMEM(bias.shape, jnp.float32),
            pltpu.VMEM((length, 2 * chan), jnp.bfloat16),
            pltpu.VMEM((2 * chan, sources * lanes), jnp.bfloat16),
        ],
    )(seq_length, tile_counts, gathered, bias, weights, w_out)


def per_device(
    pair, seq_length, tile_counts, ln_gain, w_query, w_key, w_value, w_gate, w_bias, w_out
):
    rows = pair.shape[0]
    bias_cols = jnp.repeat(w_bias, rows, axis=1)
    wcat = jnp.stack([w.T for w in (w_query, w_key, w_value, w_gate, bias_cols)])
    gathered, bias, weights = exchange(
        pair, ln_gain[None, :], wcat, lax.axis_size("keys"), lax.axis_size("heads")
    )
    return attend(seq_length, tile_counts, gathered, bias, weights, w_out)


def solution(mesh):
    in_specs = (
        P(("groups", "rows"), "keys", None),
        P("groups"),
        P(("groups", "rows"), None),
        P(),
        P(None, "heads"),
        P(None, "heads"),
        P(None, "heads"),
        P(None, "heads"),
        P(None, "heads"),
        P(),
    )
    out_specs = P(("groups", "rows"), ("keys", "heads"), None)
    return jax.shard_map(
        per_device, mesh=mesh, in_specs=in_specs, out_specs=out_specs, check_vma=False
    )
```

time: 323 us -> 234 us (0.72)
  the two profiles are of different devices: /device:TPU:33 before, /device:TPU:44 now
where the time goes in v1:
time: 234 us
  Pallas kernels  227 us (97%)
  local copies, waits for them, and re-layouts  5.55 us (2%)
    pallas_call x1, Pallas kernels, exchange(): pl.pallas_call(exchange_kernel, name='exchange', out_shape=(jax.ShapeDtyp...  140 us
    pallas_call x1, Pallas kernels, attend(): pl.pallas_call(attend_kernel, name='attend', grid=(rows,), out_shape=jax....  87.6 us
    unnamed x7, local copies, waits for them, and re-layouts  4.89 us

profile of v1, /device:TPU:44, one launch (start us, length us, event | category | flops | bytes accessed | tf_op | source)
XLA Modules:
  0.0 233.7 jit_solution(3318516343411670674)
XLA Ops:
  0.7 1.4 copy.11.counts_ref
  2.0 0.7 broadcast_in_dim.7
  2.7 0.7 bitcast_dynamic-update-slice_fusion.3
  3.4 0.7 bitcast_dynamic-update-slice_fusion.2
  4.1 0.7 bitcast_dynamic-update-slice_fusion.1
  4.8 0.7 bitcast_dynamic-update-slice_fusion
  5.6 0.0 copy-start
  5.6 0.6 copy-done
  6.2 139.8 %exchange.1 = (bf16[8,32,128,128]{3,2,1,0:T(8,128)(2,1)}, bf16[4,1024,128]{2,1,0:T(8,128)(2,1)}, bf16[2,5,64,128]{3,2,1,0:T(8,128)(2,1)}) custom-call(bf16[32,256,128]{2,1,0:T(8,128)(2,1)} %pair_ref.1, f32[1,128]{1,0:T(1,128)} %bitcast.23, bf16[5,64,128]{2,1,0:T(8,128)(2,1)} %copy-done), custom_call_target="tpu_custom_call" | custom-call | tf_op jit(solution)/shard_map/exchange/pallas_call | solution.py:303
  146.1 87.6 %attend.1 = bf16[32,128,128]{2,1,0:T(8,128)(2,1)} custom-call(s32[1]{0:T(128)S(6)} %copy.16.seq_ref, s32[32,8]{1,0:T(8,128)} %copy.11.counts_ref, bf16[8,32,128,128]{3,2,1,0:T(8,128)(2,1)} %get-tuple-element.8.g_ref, bf16[4,1024,128]{2,1,0:T(8,128)(2,1)} %get-tuple-element.9.bias_ref, bf16[2,5,64,128]{3,2,1,0:T(8,128)(2,1)} %get-tuple-element.10.w_ref, ...), custom_call_target="tpu_custom_call" | custom-call | tf_op jit(solution)/shard_map/attend/pallas_call | solution.py:388
  (1 shorter events, 0.0 us)
Async XLA Ops:
  5.6 0.6 copy-start
